TPU v7x, 32 devices: a whole 2x2x4 slice. The times are simulated.
32 devices in a mesh: bank: 4 (over x, core), zero: 8 (over z, y).
Axes of the slice: x: 2, y: 2, z: 4, core: 2. Of those that a mesh axis runs over, the one named last changes fastest.
Arguments:
- w_gate: float32 [64, 2048, 1024], P('bank', 'zero'), may hold values from -0.1875 to 0.1875
- avg_gate: float32 [64, 2048, 1024], P('bank', 'zero'), may hold values from -0.125 to 0.125
- w_up: float32 [64, 2048, 1024], P('bank', 'zero'), may hold values from -0.1875 to 0.1875
- avg_up: float32 [64, 2048, 1024], P('bank', 'zero'), may hold values from -0.125 to 0.125
- mix_share: float32 [64], P('bank'), may hold values from 0.2 to 0.8
- router_weight: float32 [2048, 64], P('zero', 'bank'), may hold values from -0.125 to 0.125
- router_gain: float32 [2048], P('zero'), may hold values from 0.25 to 1.75
Outputs:
- serve_gate: bfloat16 [64, 2048, 1024], P('bank', None, 'zero')
- serve_up: bfloat16 [64, 2048, 1024], P('bank', None, 'zero')
- scale_gate: float32 [64, 1024], P('bank', 'zero')
- scale_up: float32 [64, 1024], P('bank', 'zero')
- serve_router: bfloat16 [2048, 64], replicated
All inputs are finite; a program needn't handle non-finite values. Where the computation divides by a largest or mean magnitude, that divisor is 1e-20 or more.
Results may differ from a plain program's by a relative error of at most 0.001.
Values may be sent and summed in bfloat16 or wider, within the bound.
A program may use at most 256 MiB of HBM per device.

v0:
```python
import jax
import jax.numpy as jnp
from jax import lax
from jax.sharding import PartitionSpec as P

D_MODEL = 2048


def on_device(w_gate, avg_gate, w_up, avg_up, mix_share, router_weight, router_gain):
    fresh_gate = mix_share[:, None, None] * w_gate + (1.0 - mix_share[:, None, None]) * avg_gate
    fresh_up = mix_share[:, None, None] * w_up + (1.0 - mix_share[:, None, None]) * avg_up
    total_gate, total_up = lax.psum(
        (jnp.sum(jnp.abs(fresh_gate), axis=1), jnp.sum(jnp.abs(fresh_up), axis=1)), "zero"
    )
    scale_gate = total_gate / D_MODEL
    scale_up = total_up / D_MODEL
    narrow_gate, narrow_up = (
        (fresh_gate / jnp.expand_dims(scale_gate, 1)).astype(jnp.bfloat16),
        (fresh_up / jnp.expand_dims(scale_up, 1)).astype(jnp.bfloat16),
    )
    serve_gate, serve_up = (
        lax.all_to_all(narrow_gate, "zero", split_axis=2, concat_axis=1, tiled=True),
        lax.all_to_all(narrow_up, "zero", split_axis=2, concat_axis=1, tiled=True),
    )
    scale_gate = lax.dynamic_slice_in_dim(
        scale_gate, lax.axis_index("zero") * serve_gate.shape[2], serve_gate.shape[2], axis=1
    )
    scale_up = lax.dynamic_slice_in_dim(
        scale_up, lax.axis_index("zero") * serve_up.shape[2], serve_up.shape[2], axis=1
    )
    part_router = (router_weight * router_gain[:, None]).astype(jnp.bfloat16)
    row_router = lax.all_gather(part_router, "zero", axis=0, tiled=True)
    serve_router = lax.all_gather(row_router, "bank", axis=1, tiled=True)
    return (serve_gate, serve_up, scale_gate, scale_up, serve_router)


def solution(mesh):
    in_specs = (
        P("bank", "zero", None),
        P("bank", "zero", None),
        P("bank", "zero", None),
        P("bank", "zero", None),
        P("bank"),
        P("zero", "bank"),
        P("zero"),
    )
    out_specs = (
        P("bank", None, "zero"),
        P("bank", None, "zero"),
        P("bank", "zero"),
        P("bank", "zero"),
        P(),
    )
    return jax.shard_map(
        on_device, mesh=mesh, in_specs=in_specs, out_specs=out_specs, check_vma=False
    )
```

profile of v0, /device:TPU:0, one launch (start us, length us, event | category | flops | bytes accessed | tf_op | source)
XLA Modules:
  0.0 642.4 jit_solution(310486662684483789)
XLA Ops:
  7.2 0.0 all-reduce.3.cloned.1.call-start
  7.2 17.6 %copy.22 = f32[16,256,1024]{1,0,2:T(8,128)} copy(f32[16,256,1024]{2,1,0:T(8,128)} %param.7) | data formatting | bytes 33554432 | tf_op args[0]
  24.8 17.6 %copy.23 = f32[16,256,1024]{1,0,2:T(8,128)} copy(f32[16,256,1024]{2,1,0:T(8,128)} %param.8) | data formatting | bytes 33554432 | tf_op args[1]
  42.4 17.6 %copy.25 = f32[16,256,1024]{1,0,2:T(8,128)} copy(f32[16,256,1024]{2,1,0:T(8,128)} %param.9) | data formatting | bytes 33554432 | tf_op args[2]
  60.0 0.0 copy-start.1
  60.0 17.6 %copy.26 = f32[16,256,1024]{1,0,2:T(8,128)} copy(f32[16,256,1024]{2,1,0:T(8,128)} %param.10) | data formatting | bytes 33554432 | tf_op args[3]
  77.6 0.0 copy-done.1
  77.6 23.7 %abs_reduce_fusion = (f32[16,1024]{0,1:T(8,128)}, f32[16,1024]{0,1:T(8,128)}) fusion(f32[16,256,1024]{1,0,2:T(8,128)} %copy.26, f32[16]{0:T(128)S(1)} %broadcast_subtract_fusion, f32[16,256,1024]{1,0,2:T(8,128)} %copy.25, f32[16]{0:T(128)S(1)} %copy-done.1, f32[16,256,1024]{1,0,2:T(8,128)} %copy.23, f32[16,256,1024]{1,0,2:T(8,128)} %copy.22), kind=kLoop, calls=%fused_computation.1 | loop fusion | flops 41910272 | bytes 67240064 | tf_op jit(solution)/shard_map/reduce_sum | solution.py:13
  101.3 0.0 all-reduce.3.cloned.1.call-update
  101.4 81.1 %all-reduce.3.cloned.1.call-done = (f32[16,1024]{0,1:T(8,128)}, f32[16,1024]{0,1:T(8,128)}) async-done(((f32[16,1024]{0,1:T(8,128)}, f32[16,1024]{0,1:T(8,128)}), (f32[16,1024]{0,1:T(8,128)}, f32[16,1024]{0,1:T(8,128)})) %all-reduce.3.cloned.1.call-update) | async-done | bytes 131088 | tf_op jit(solution)/shard_map/psum | solution.py:12
  182.5 1.3 broadcast_multiply_fusion
  183.8 25.3 %divide_convert_fusion = (bf16[16,256,1024]{1,0,2:T(8,128)(2,1)}, bf16[16,256,1024]{1,0,2:T(8,128)(2,1)S(1)}) fusion(f32[16,1024]{0,1:T(8,128)S(1)} %get-tuple-element.16, f32[16,256,1024]{1,0,2:T(8,128)} %copy.26, f32[16]{0:T(128)S(1)} %broadcast_subtract_fusion, f32[16,256,1024]{1,0,2:T(8,128)} %copy.25, f32[16]{0:T(128)S(1)} %copy-done.1, ...), kind=kLoop, calls=%fused_computation | loop fusion | flops 41943040 | bytes 84017280 | tf_op jit(solution)/shard_map/convert_element_type | solution.py:19
  209.1 187.1 %all_to_all.36 = bf16[16,256,1024]{1,0,2:T(8,128)(2,1)} all-to-all(bf16[16,256,1024]{1,0,2:T(8,128)(2,1)S(1)} %get-tuple-element.15), channel_id=1, replica_groups=mesh['bank'=4,'zero'=8] {'zero'}, dimensions={2} | all-to-all | bytes 16777216 | tf_op jit(solution)/shard_map/all_to_all | solution.py:22
  396.2 4.9 all-to-all-start.1
  401.1 0.0 copy-done
  401.1 0.0 copy-done.2
  401.1 202.0 %all_gather.6 = bf16[2048,16]{0,1:T(8,128)(2,1)S(1)} all-gather(bf16[256,16]{0,1:T(8,128)(2,1)S(1)} %multiply_convert_fusion), channel_id=1, replica_groups=mesh['bank'=4,'zero'=8] {'zero'}, dimensions={0}, use_global_device_ids=true | all-gather | bytes 73728 | tf_op jit(solution)/shard_map/all_gather | solution.py:32
  603.2 5.8 all_gather.7
  608.9 0.7 copy.28
  609.6 0.7 copy.29
  610.3 12.3 %copy.24 = bf16[16,8,256,128]{3,2,1,0:T(8,128)(2,1)} copy(bf16[16,8,256,128]{2,0,3,1:T(8,128)(2,1)} %bitcast.8) | data formatting | bytes 16777216 | tf_op jit(solution)/shard_map/all_to_all | solution.py:22
  622.6 0.0 all-to-all-done.1
  622.6 12.3 %copy.27 = bf16[16,8,256,128]{3,2,1,0:T(8,128)(2,1)} copy(bf16[16,8,256,128]{2,0,3,1:T(8,128)(2,1)} %bitcast.4) | data formatting | bytes 16777216 | tf_op jit(solution)/shard_map/all_to_all | solution.py:23
  634.8 0.7 copy.33
  (6 shorter events, 0.0 us)
Async XLA Ops:
  7.2 175.3 %all-reduce.3.cloned.1.call-start = ((), (), s32[]{:S(2)}) async-start(), calls=%async_computation.2 | async-start | bytes 2097152 | tf_op jit(solution)/shard_map/psum | solution.py:12
  60.0 17.6 %copy-start.1 = (f32[16]{0:T(128)S(1)}, f32[16]{0:T(128)}, u32[]{:S(2)}) copy-start(f32[16]{0:T(128)} %param.11) | copy-start | bytes 196
  209.1 192.0 %copy-start = (f32[256,16]{0,1:T(8,128)S(1)}, f32[256,16]{0,1:T(8,128)}, u32[]{:S(2)}) copy-start(f32[256,16]{0,1:T(8,128)} %param.12) | copy-start | bytes 49156
  209.1 192.0 %copy-start.2 = (f32[256]{0:T(256)S(1)}, f32[256]{0:T(256)}, u32[]{:S(2)}) copy-start(f32[256]{0:T(256)} %param.13) | copy-start | bytes 3076
  396.2 226.4 %all-to-all-start.1 = ((bf16[16,256,1024]{1,0,2:T(8,128)(2,1)}), bf16[16,256,1024]{1,0,2:T(8,128)(2,1)}, u32[]{:S(2)}, u32[]{:S(2)}) async-start(bf16[16,256,1024]{1,0,2:T(8,128)(2,1)} %get-tuple-element.14), calls=%async_computation.1 | async-start | bytes 16777216 | tf_op jit(solution)/shard_map/all_to_all | solution.py:23
Sparse Core Ops, SparseCore 0:
  101.5 80.9 all-reduce.2
where the time goes:
time: 644 us; the launch traced here: 642 us
  blocking collectives  395 us (61%)
  local copies, waits for them, and re-layouts  97 us (15%)
  waiting for transfers between devices  81.2 us (13%)
  other arithmetic  50.3 us (8%)
  between operations  14.1 us (2%)
    all_gather x1, blocking collectives, on_device(): row_router = lax.all_gather(part_router, 'zero', axis=0, tiled=True)  202 us
    all_to_all x1, blocking collectives, on_device(): lax.all_to_all(narrow_gate, 'zero', split_axis=2, concat_axis=1, tiled=True)  187 us
    psum x1, waiting for transfers between devices, on_device(): lax.psum((jnp.sum(jnp.abs(fresh_gate), axis=1), jnp.sum(jnp.abs(fresh_up)...  81.1 us
    unnamed x13, local copies, waits for them, and re-layouts  72.5 us
    convert_element_type x1, other arithmetic, on_device(): (fresh_up / jnp.expand_dims(scale_up, 1)).astype(jnp.bfloat16)  25.3 us
    reduce_sum x1, other arithmetic, on_device(): jnp.sum(jnp.abs(fresh_up), axis=1)  23.7 us
  transfers between devices with their start and end apart: 2, of which 1 were waited for; matrix products, arithmetic and copies ran while one was open for 2% of the time, Pallas kernels for 0%

commit v1 on v0

--- a/solution.py
+++ b/solution.py
@@ -19,7 +19,12 @@
         (fresh_up / jnp.expand_dims(scale_up, 1)).astype(jnp.bfloat16),
     )
     serve_gate, serve_up = (
-        lax.all_to_all(narrow_gate, "zero", split_axis=2, concat_axis=1, tiled=True),
+        jnp.concatenate(
+            lax.all_to_all(
+                jnp.stack(jnp.split(narrow_gate, lax.axis_size("zero"), axis=2)), "zero", 0, 0
+            ),
+            axis=1,
+        ),
         lax.all_to_all(narrow_up, "zero", split_axis=2, concat_axis=1, tiled=True),
     )
     scale_gate = lax.dynamic_slice_in_dim(

time: 644 us -> 577 us (0.90)
  blocking collectives: 395 us -> 208 us
  waiting for transfers between devices: 81.2 us -> 240 us
  local copies, waits for them, and re-layouts: 97 us -> 49.8 us
    all_to_all x1 -> x0, blocking collectives: 187 us -> none  [on_device(): lax.all_to_all(narrow_gate, 'zero', split_axis=2, concat_axis=1, tiled=True)]
    all_to_all x1, waiting for transfers between devices: 0.01 us -> 166 us  [on_device(): lax.all_to_all(narrow_up, 'zero', split_axis=2, concat_axis=1, tiled=True)]
    unnamed x13 -> x16, local copies, waits for them, and re-layouts: 72.5 us -> 14.6 us
    convert_element_type x0 -> x1, local copies, waits for them, and re-layouts: none -> 12.6 us  [on_device(): (fresh_up / jnp.expand_dims(scale_up, 1)).astype(jnp.bfloat16)]
    psum x1, waiting for transfers between devices: 81.1 us -> 73.6 us  [on_device(): lax.psum((jnp.sum(jnp.abs(fresh_gate), axis=1), jnp.sum(jnp.abs(fresh_up)...]
  transfers between devices with their start and end apart: 2 -> 3, of which waited for: 1 -> 2; matrix products, arithmetic and copies ran while one was open for 2% -> 5% of each run, Pallas kernels for 0% -> 0%
where the time goes in v1:
time: 577 us; the launch traced here: 576 us
  waiting for transfers between devices  240 us (42%)
  blocking collectives  208 us (36%)
  other arithmetic  54.3 us (9%)
  local copies, waits for them, and re-layouts  49.8 us (9%)
  between operations  14.1 us (2%)
  starting transfers between devices  9.99 us (2%)
    all_gather x1, blocking collectives, on_device(): row_router = lax.all_gather(part_router, 'zero', axis=0, tiled=True)  202 us
    all_to_all x1, waiting for transfers between devices, on_device(): lax.all_to_all(narrow_up, 'zero', split_axis=2, concat_axis=1, tiled=True)  166 us
    psum x1, waiting for transfers between devices, on_device(): lax.psum((jnp.sum(jnp.abs(fresh_gate), axis=1), jnp.sum(jnp.abs(fresh_up)...  73.6 us
    convert_element_type x1, other arithmetic, on_device(): (fresh_up / jnp.expand_dims(scale_up, 1)).astype(jnp.bfloat16)  29.4 us
    reduce_sum x1, other arithmetic, on_device(): jnp.sum(jnp.abs(fresh_up), axis=1)  23.3 us
    unnamed x16, local copies, waits for them, and re-layouts  14.6 us
    convert_element_type x1, local copies, waits for them, and re-layouts, on_device(): (fresh_up / jnp.expand_dims(scale_up, 1)).astype(jnp.bfloat16)  12.6 us
    all_to_all x1, local copies, waits for them, and re-layouts, on_device(): lax.all_to_all(narrow_up, 'zero', split_axis=2, concat_axis=1, tiled=True)  12.3 us
  transfers between devices with their start and end apart: 3, of which 2 were waited for; matrix products, arithmetic and copies ran while one was open for 5% of the time, Pallas kernels for 0%

profile of v1, /device:TPU:0, one launch (start us, length us, event | category | flops | bytes accessed | tf_op | source)
XLA Modules:
  0.0 575.6 jit_solution(11192683282633137872)
XLA Ops:
  7.2 0.7 broadcast_subtract_fusion
  7.9 23.3 %abs_reduce_fusion = (f32[16,1024]{1,0:T(8,128)}, f32[16,1024]{1,0:T(8,128)}) fusion(f32[16,256,1024]{2,1,0:T(8,128)} %param.10, f32[16]{0:T(128)S(1)} %broadcast_subtract_fusion, f32[16,256,1024]{2,1,0:T(8,128)} %param.9, f32[16]{0:T(128)} %param.11, f32[16,256,1024]{2,1,0:T(8,128)} %param.8, f32[16,256,1024]{2,1,0:T(8,128)} %param.7), kind=kLoop, calls=%fused_computation.1 | loop fusion | flops 41910272 | bytes 67240064 | tf_op jit(solution)/shard_map/reduce_sum | solution.py:13
  31.2 73.6 %all-reduce.3.cloned.1.call-done = (f32[16,1024]{1,0:T(8,128)}, f32[16,1024]{1,0:T(8,128)}) async-done(((f32[16,1024]{1,0:T(8,128)}, f32[16,1024]{1,0:T(8,128)}), (f32[16,1024]{1,0:T(8,128)}, f32[16,1024]{1,0:T(8,128)})) %all-reduce.3.cloned.1.call-update) | async-done | bytes 131088 | tf_op jit(solution)/shard_map/psum | solution.py:12
  104.8 0.9 broadcast_multiply_fusion
  105.7 29.4 %divide_convert_fusion = (bf16[16,256,1024]{2,1,0:T(8,128)(2,1)}, bf16[16,256,1024]{2,1,0:T(8,128)(2,1)}) fusion(f32[16,1024]{1,0:T(8,128)S(1)} %get-tuple-element.11, f32[16,256,1024]{2,1,0:T(8,128)} %param.10, f32[16]{0:T(128)S(1)} %broadcast_subtract_fusion, f32[16,256,1024]{2,1,0:T(8,128)} %param.9, f32[16]{0:T(128)S(1)} %copy-done.2, ...), kind=kLoop, calls=%fused_computation | loop fusion | flops 41943040 | bytes 84017280 | tf_op jit(solution)/shard_map/convert_element_type | solution.py:19
  135.1 12.6 %copy.31 = bf16[16,256,1024]{1,0,2:T(8,128)(2,1)} copy(bf16[16,256,1024]{2,1,0:T(8,128)(2,1)} %get-tuple-element.9) | data formatting | bytes 16777216 | tf_op jit(solution)/shard_map/convert_element_type | solution.py:19
  147.7 4.9 all-to-all-start.1
  152.6 2.4 fusion.7
  155.1 3.0 fusion.6
  158.1 2.3 fusion.5
  160.4 2.3 fusion.4
  162.7 1.2 fusion.3
  163.9 1.3 fusion.2
  165.2 1.3 fusion.1
  166.5 1.3 fusion
  167.8 166.2 %all-to-all-done.1 = bf16[16,256,1024]{1,0,2:T(8,128)(2,1)} async-done(((bf16[16,256,1024]{1,0,2:T(8,128)(2,1)}), bf16[16,256,1024]{1,0,2:T(8,128)(2,1)}, u32[]{:S(2)}, u32[]{:S(2)}) %all-to-all-start.1) | async-done | bytes 8388640 | tf_op jit(solution)/shard_map/all_to_all | solution.py:28
  334.0 5.0 all-to-all-start
  339.0 201.9 %all_gather.6 = bf16[2048,16]{0,1:T(8,128)(2,1)S(1)} all-gather(bf16[256,16]{0,1:T(8,128)(2,1)S(1)} %multiply_convert_fusion), channel_id=1, replica_groups=mesh['bank'=4,'zero'=8] {'zero'}, dimensions={0}, use_global_device_ids=true | all-gather | bytes 73728 | tf_op jit(solution)/shard_map/all_gather | solution.py:37
  540.9 5.8 %all_gather.7 = bf16[2048,64]{0,1:T(8,128)(2,1)S(1)} all-gather(bf16[2048,16]{0,1:T(8,128)(2,1)S(1)} %all_gather.6), channel_id=1, replica_groups=mesh['bank'=4,'zero'=8] {'bank'}, dimensions={1}, use_global_device_ids=true | all-gather | bytes 327680 | tf_op jit(solution)/shard_map/all_gather | solution.py:38
  546.7 0.6 constant_dynamic-slice_fusion
  547.3 0.6 constant_dynamic-slice_fusion.1
  547.9 12.3 %copy.32 = bf16[16,8,256,128]{3,2,1,0:T(8,128)(2,1)} copy(bf16[16,8,256,128]{2,0,3,1:T(8,128)(2,1)} %bitcast.11) | data formatting | bytes 16777216 | tf_op jit(solution)/shard_map/all_to_all | solution.py:28
  560.2 7.9 %copy.30 = bf16[8,16,256,128]{3,2,0,1:T(8,128)(2,1)} copy(bf16[8,16,256,128]{3,2,1,0:T(8,128)(2,1)} %all-to-all-done) | data formatting | bytes 16777216 | tf_op jit(solution)/shard_map/all_to_all | solution.py:23
  568.1 0.7 copy.43
  (12 shorter events, 0.1 us)
Async XLA Ops:
  7.2 97.6 %all-reduce.3.cloned.1.call-start = ((), (), s32[]{:S(2)}) async-start(), calls=%async_computation.2 | async-start | bytes 262144 | tf_op jit(solution)/shard_map/psum | solution.py:12
  7.9 97.8 %copy-start.2 = (f32[16]{0:T(128)S(1)}, f32[16]{0:T(128)}, u32[]{:S(2)}) copy-start(f32[16]{0:T(128)} %param.11) | copy-start | bytes 196
  147.7 186.3 %all-to-all-start.1 = ((bf16[16,256,1024]{1,0,2:T(8,128)(2,1)}), bf16[16,256,1024]{1,0,2:T(8,128)(2,1)}, u32[]{:S(2)}, u32[]{:S(2)}) async-start(bf16[16,256,1024]{1,0,2:T(8,128)(2,1)} %copy.31), calls=%async_computation.1 | async-start | bytes 16777216 | tf_op jit(solution)/shard_map/all_to_all | solution.py:28
  152.6 10.1 %copy-start = (bf16[16,256,1024]{2,1,0:T(8,128)(2,1)S(1)}, bf16[16,256,1024]{2,1,0:T(8,128)(2,1)}, u32[]{:S(2)}) copy-start(bf16[16,256,1024]{2,1,0:T(8,128)(2,1)} %get-tuple-element.10) | copy-start | bytes 25165828
  167.8 171.2 %copy-start.1 = (f32[256,16]{0,1:T(8,128)S(1)}, f32[256,16]{0,1:T(8,128)}, u32[]{:S(2)}) copy-start(f32[256,16]{0,1:T(8,128)} %param.12) | copy-start | bytes 49156
  167.8 171.2 %copy-start.3 = (f32[256]{0:T(256)S(1)}, f32[256]{0:T(256)}, u32[]{:S(2)}) copy-start(f32[256]{0:T(256)} %param.13) | copy-start | bytes 3076
  334.0 226.2 %all-to-all-start = ((bf16[8,16,256,128]{3,2,1,0:T(8,128)(2,1)}), bf16[8,16,256,128]{3,2,1,0:T(8,128)(2,1)}, u32[]{:S(2)}, u32[]{:S(2)}) async-start(bf16[8,16,256,128]{3,2,1,0:T(8,128)(2,1)} %fusion), calls=%async_computation | async-start | bytes 16777216 | tf_op jit(solution)/shard_map/all_to_all | solution.py:23
Sparse Core Ops, SparseCore 0:
  31.3 73.4 all-reduce.2
